TPU v7x, 256 devices: a whole 4x4x8 slice. The times are simulated.
256 devices in a mesh: prow: 8 (over z), pcol: 32 (over y, x, core).
Axes of the slice: x: 4, y: 4, z: 8, core: 2. Of those that a mesh axis runs over, the one named last changes fastest.
Arguments:
- points: float32 [1, 32, 2, 1024], P(None, 'pcol'), may hold values from 0 to 1
- range_length: float32 [1], replicated, may hold values from 0.05 to 0.15
- smoothness: int32 [1], replicated, may hold values from 0 to 2
- sketch_bank: bfloat16 [32, 48, 1024], P('pcol'), may hold values from -6 to 6
- sketch_ids: int32 [4, 8, 1, 32], P(None, 'prow', None, 'pcol'), may hold values from 0 to 31
- tile_ranks: int32 [4, 8, 1, 32], P(None, 'prow', None, 'pcol'), may hold values from 16 to 48
Outputs:
- y_factors: float32 [4, 8, 1, 32, 48, 1024], P(None, 'prow', None, 'pcol')
- c_factors: float32 [4, 8, 1, 32, 48, 1024], P(None, 'prow', None, 'pcol')
- tile_error: float32 [4, 8, 1, 32], P(None, 'prow', None, 'pcol')
- rank_total: int32 [1], replicated
All inputs are finite; a program needn't handle non-finite values.
Results may differ from a plain program's by a relative error of at most 0.0098.
The roundings to bfloat16 on the way count: a program that leaves them out, or rounds other values in their place, can miss the bound.
Values may be sent and summed in bfloat16 or wider, within the bound.
A program may use at most 64 MiB of HBM per device.

v0:
```python
import jax
import jax.numpy as jnp
from jax import lax
from jax.sharding import Mesh
from jax.sharding import PartitionSpec as P

PCOL = ("pcol_0", "pcol_1", "pcol_2")
PROW_PCOL = ("prow", "pcol_0", "pcol_1", "pcol_2")


def joined_along(parts, dim):
    shape = list(parts.shape[1:])
    shape[dim] *= parts.shape[0]
    return jnp.moveaxis(parts, 0, dim).reshape(shape)


def sent_to_all(x, axis):
    copies = jnp.broadcast_to(x, (lax.axis_size(axis), *x.shape))
    return lax.all_to_all(copies, axis, split_axis=0, concat_axis=0, tiled=True)


def collect(x, axis, dim):
    return joined_along(sent_to_all(x, axis), dim)


def one_axis_at_a_time(x, axes):
    for axis in axes:
        x = lax.psum(x, axis)
    return x


def kernel_factors(smoothness, range_length):
    morton_value = smoothness[0].astype(jnp.float32)
    kernel_scale = jnp.sqrt(2.0 * morton_value + 1.0) / range_length[0]
    linear_factor = jnp.where(smoothness[0] >= 1, 1.0, 0.0).astype(jnp.float32)
    squared_distance = jnp.where(smoothness[0] >= 2, 1.0 / 3.0, 0.0).astype(jnp.float32)
    return (kernel_scale, linear_factor, squared_distance)


def covariance_tile(row_locations, column_locations, kernel_scale, linear_factor, squared_distance):
    offset_horizontal = row_locations[0][:, None] - column_locations[0][None, :]
    offset_vertical = row_locations[1][:, None] - column_locations[1][None, :]
    scaled_distance = kernel_scale * jnp.sqrt(
        offset_horizontal * offset_horizontal + offset_vertical * offset_vertical
    )
    return (
        1.0 + linear_factor * scaled_distance + squared_distance * scaled_distance * scaled_distance
    ) * jnp.exp(-scaled_distance)


def compress(tile_low, sketch, rank):
    keep = jnp.arange(sketch.shape[0]) < rank
    sketch = jnp.where(keep[:, None], sketch, jnp.zeros_like(sketch))
    sketched = lax.dot_general(
        sketch, tile_low, (((1,), (1,)), ((), ())), preferred_element_type=jnp.float32
    )
    product = jnp.dot(sketched.astype(jnp.bfloat16), tile_low, preferred_element_type=jnp.float32)
    gram = jnp.dot(sketched, sketched.T, precision=lax.Precision.HIGHEST)
    shift = 0.1 * jnp.trace(gram) / rank.astype(jnp.float32)
    gram = gram + jnp.diag(jnp.where(keep, shift, jnp.ones_like(shift)))
    factor = jnp.linalg.cholesky(gram)
    coeffs = jax.scipy.linalg.cho_solve((factor, True), product)
    approx = lax.dot_general(
        sketched, coeffs, (((0,), (0,)), ((), ())), precision=lax.Precision.HIGHEST
    )
    error = tile_low.astype(jnp.float32) - approx
    return (sketched, coeffs, jnp.sum(error * error))


def per_device(points, range_length, smoothness, sketch_bank, sketch_ids, tile_ranks):
    row_count = lax.axis_size("prow")
    col_count = lax.axis_size(PCOL)
    row_place = lax.axis_index("prow")
    col_place = lax.axis_index(PCOL)
    row_tiles = sketch_ids.shape[0]
    col_tiles = sketch_ids.shape[2]
    tile_size = points.shape[3]
    sketch_rows = sketch_bank.shape[1]
    slots_total = row_tiles * col_tiles
    tiles_across = col_tiles * col_count
    kernel_scale, linear_factor, squared_distance = kernel_factors(smoothness, range_length)
    gathered = collect(points, PCOL, 1)
    every_block = gathered.reshape(tiles_across, 2, tile_size)
    row_index = jnp.arange(row_tiles, dtype=jnp.int32) * row_count + row_place
    col_index = jnp.arange(col_tiles, dtype=jnp.int32) * col_count + col_place
    slot_row = jnp.repeat(row_index, col_tiles)
    slot_col = jnp.tile(col_index, row_tiles)
    own_ids = sketch_ids.reshape(slots_total)
    own_ranks = tile_ranks.reshape(slots_total)
    lower = slot_col <= slot_row
    offdiag = slot_col < slot_row
    ranks_local = jnp.sum(jnp.where(offdiag, own_ranks, 0))
    rank_sum = one_axis_at_a_time(ranks_local, PROW_PCOL)
    bank_whole = lax.all_gather(sketch_bank, PCOL, axis=0, tiled=True)
    chosen = bank_whole[own_ids]
    row_points_all = every_block[slot_row]
    col_points_all = every_block[slot_col]

    def one_tile(row_locations, column_locations, sketch, rank):
        tile_block = covariance_tile(
            row_locations, column_locations, kernel_scale, linear_factor, squared_distance
        )
        norm_sq = jnp.sum(tile_block * tile_block)
        sketched, coeffs, err_sq = compress(tile_block.astype(jnp.bfloat16), sketch, rank)
        return (sketched, coeffs, norm_sq, err_sq)

    def mapped(inputs):
        return one_tile(inputs[0], inputs[1], inputs[2], inputs[3])

    sketched_all, coeffs_all, norm_all, err_all = lax.map(
        mapped, (row_points_all, col_points_all, chosen, own_ranks)
    )
    norm_local = jnp.sum(jnp.where(lower, jnp.where(offdiag, 2.0, 1.0) * norm_all, 0.0))
    total = one_axis_at_a_time(norm_local, PROW_PCOL)
    errors = (
        jnp.where(offdiag, jnp.sqrt(err_all), jnp.sqrt(norm_all)) * tiles_across / jnp.sqrt(total)
    )
    errors = jnp.where(lower, errors, 0.0)
    out_shape = (row_tiles, 1, col_tiles, 1, sketch_rows, tile_size)
    y_out = jnp.where(offdiag[:, None, None], sketched_all, 0.0).reshape(out_shape)
    c_out = jnp.where(offdiag[:, None, None], coeffs_all, 0.0).reshape(out_shape)
    err_out = errors.reshape(row_tiles, 1, col_tiles, 1)
    rank_out = rank_sum.reshape(1)
    return (y_out, c_out, err_out, rank_out)


def solution(mesh):
    split = Mesh(
        mesh.devices.reshape(mesh.shape["prow"], 4, 4, 2), ("prow", "pcol_0", "pcol_1", "pcol_2")
    )
    placed = (
        P(None, PCOL, None, None),
        P(),
        P(),
        P(PCOL, None, None),
        P(None, "prow", None, PCOL),
        P(None, "prow", None, PCOL),
    )
    return jax.shard_map(
        per_device,
        mesh=split,
        in_specs=placed,
        out_specs=(
            P(None, "prow", None, PCOL, None, None),
            P(None, "prow", None, PCOL, None, None),
            P(None, "prow", None, PCOL),
            P(),
        ),
        check_vma=False,
    )
```

profile of v0, /device:TPU:1, one launch (start us, length us, event | category | flops | bytes accessed | tf_op | source)
XLA Modules:
  0.0 285.3 jit_solution(14311572031564186619)
XLA Ops:
  9.4 8.6 %all-to-all-start = ((f32[32,1,1,2,1024]{4,3,2,1,0:T(2,128)}), f32[32,1,1,2,1024]{4,3,2,1,0:T(2,128)S(1)}, u32[]{:S(2)}, u32[]{:S(2)}) async-start(f32[32,1,1,2,1024]{4,3,2,1,0:T(2,128)} %broadcast_in_dim.93), calls=%async_computation | async-start | bytes 524288 | tf_op jit(solution)/shard_map/all_to_all | solution.py:19
  21.4 5.4 %all-to-all-done = f32[32,1,1,2,1024]{4,3,2,1,0:T(2,128)S(1)} async-done(((f32[32,1,1,2,1024]{4,3,2,1,0:T(2,128)}), f32[32,1,1,2,1024]{4,3,2,1,0:T(2,128)S(1)}, u32[]{:S(2)}, u32[]{:S(2)}) %all-to-all-start) | async-done | bytes 262176 | tf_op jit(solution)/shard_map/all_to_all | solution.py:19
  28.0 36.6 %all-gather.2.cloned.1.call-done = bf16[32,48,1024]{2,1,0:T(8,128)(2,1)} async-done(((bf16[1,48,1024]{2,1,0:T(8,128)(2,1)}), bf16[32,48,1024]{2,1,0:T(8,128)(2,1)}) %all-gather.2.cloned.1.call-update) | async-done | bytes 3145744 | tf_op jit(solution)/shard_map/all_gather | solution.py:94
  67.2 136.1 %while.17 = (s32[]{:T(128)}, f32[4,48,1024]{2,1,0:T(8,128)S(1)}, f32[4,48,1024]{2,1,0:T(8,128)S(1)}, f32[4]{0:T(128)S(1)}, f32[4]{0:T(128)S(1)}, /*index=5*/s32[...) while((s32[]{:T(128)}, f32[4,48,1024]{2,1,0:T(8,128)S(1)}, ...), condition=%wide.region_6.7_spmd.clone, body=%wide.region_0.6_spmd.sunk.clone | while | flops 954344128 | bytes 2675283 | solution.py:110
  69.2 4.2 %multiply_reduce_fusion.6 = f32[]{:T(128)} fusion(f32[]{:T(128)} %get-tuple-element.278, f32[1024]{0:T(1024)S(1)} %bitcast.123, f32[1024]{0:T(1024)S(1)} %bitcast.127, f32[1024]{0:T(1024)S(1)} %bitcast.119, f32[1024]{0:T(1024)S(1)} %bitcast.131, f32[]{:T(128)} %get-tuple-element.275, f32[]{:T(128)} %get-tuple-element.274), kind=kLoop, calls=%fused_computation.7.clone.1.clone | loop fusion | flops 15728639 | bytes 16400 | tf_op jit(solution)/shard_map/while/body/eval_jaxpr/reduce_sum | solution.py:103
  79.9 4.4 %cholesky.73 = f32[48,48]{1,0:T(8,128)S(1)} custom-call(f32[48,48]{1,0:T(8,128)S(1)} %fusion.68), custom_call_target="Cholesky" | custom-call | tf_op jit(solution)/shard_map/while/body/eval_jaxpr/jit(cholesky)/cholesky | solution.py:61
  93.1 7.4 %multiply_reduce_fusion.7 = f32[]{:T(128)} fusion(f32[48,1024]{1,0:T(8,128)S(1)} %get-tuple-element.222, f32[48,1024]{1,0:T(8,128)S(1)} %get-tuple-element.226, f32[]{:T(128)} %get-tuple-element.278, f32[1024]{0:T(1024)S(1)} %bitcast.126, f32[1024]{0:T(1024)S(1)} %bitcast.130, f32[1024]{0:T(1024)S(1)} %bitcast.122, f32[1024]{0:T(1024)S(1)} %bitcast.134, ...), kind=kOutput, calls=%fused_computation.6.clone.1.clone | convolution fusion | flops 622854144 | bytes 409616 | tf_op jit(solution)/shard_map/while/body/eval_jaxpr/dot_general | solution.py:63
  103.2 4.2 %multiply_reduce_fusion.6 = f32[]{:T(128)} fusion(f32[]{:T(128)} %get-tuple-element.278, f32[1024]{0:T(1024)S(1)} %bitcast.123, f32[1024]{0:T(1024)S(1)} %bitcast.127, f32[1024]{0:T(1024)S(1)} %bitcast.119, f32[1024]{0:T(1024)S(1)} %bitcast.131, f32[]{:T(128)} %get-tuple-element.275, f32[]{:T(128)} %get-tuple-element.274), kind=kLoop, calls=%fused_computation.7.clone.1.clone | loop fusion | flops 15728639 | bytes 16400 | tf_op jit(solution)/shard_map/while/body/eval_jaxpr/reduce_sum | solution.py:103
  113.9 4.4 %cholesky.73 = f32[48,48]{1,0:T(8,128)S(1)} custom-call(f32[48,48]{1,0:T(8,128)S(1)} %fusion.68), custom_call_target="Cholesky" | custom-call | tf_op jit(solution)/shard_map/while/body/eval_jaxpr/jit(cholesky)/cholesky | solution.py:61
  127.2 7.4 %multiply_reduce_fusion.7 = f32[]{:T(128)} fusion(f32[48,1024]{1,0:T(8,128)S(1)} %get-tuple-element.222, f32[48,1024]{1,0:T(8,128)S(1)} %get-tuple-element.226, f32[]{:T(128)} %get-tuple-element.278, f32[1024]{0:T(1024)S(1)} %bitcast.126, f32[1024]{0:T(1024)S(1)} %bitcast.130, f32[1024]{0:T(1024)S(1)} %bitcast.122, f32[1024]{0:T(1024)S(1)} %bitcast.134, ...), kind=kOutput, calls=%fused_computation.6.clone.1.clone | convolution fusion | flops 622854144 | bytes 409616 | tf_op jit(solution)/shard_map/while/body/eval_jaxpr/dot_general | solution.py:63
  137.2 4.2 %multiply_reduce_fusion.6 = f32[]{:T(128)} fusion(f32[]{:T(128)} %get-tuple-element.278, f32[1024]{0:T(1024)S(1)} %bitcast.123, f32[1024]{0:T(1024)S(1)} %bitcast.127, f32[1024]{0:T(1024)S(1)} %bitcast.119, f32[1024]{0:T(1024)S(1)} %bitcast.131, f32[]{:T(128)} %get-tuple-element.275, f32[]{:T(128)} %get-tuple-element.274), kind=kLoop, calls=%fused_computation.7.clone.1.clone | loop fusion | flops 15728639 | bytes 16400 | tf_op jit(solution)/shard_map/while/body/eval_jaxpr/reduce_sum | solution.py:103
  147.9 4.4 %cholesky.73 = f32[48,48]{1,0:T(8,128)S(1)} custom-call(f32[48,48]{1,0:T(8,128)S(1)} %fusion.68), custom_call_target="Cholesky" | custom-call | tf_op jit(solution)/shard_map/while/body/eval_jaxpr/jit(cholesky)/cholesky | solution.py:61
  161.2 7.4 %multiply_reduce_fusion.7 = f32[]{:T(128)} fusion(f32[48,1024]{1,0:T(8,128)S(1)} %get-tuple-element.222, f32[48,1024]{1,0:T(8,128)S(1)} %get-tuple-element.226, f32[]{:T(128)} %get-tuple-element.278, f32[1024]{0:T(1024)S(1)} %bitcast.126, f32[1024]{0:T(1024)S(1)} %bitcast.130, f32[1024]{0:T(1024)S(1)} %bitcast.122, f32[1024]{0:T(1024)S(1)} %bitcast.134, ...), kind=kOutput, calls=%fused_computation.6.clone.1.clone | convolution fusion | flops 622854144 | bytes 409616 | tf_op jit(solution)/shard_map/while/body/eval_jaxpr/dot_general | solution.py:63
  171.2 4.2 %multiply_reduce_fusion.6 = f32[]{:T(128)} fusion(f32[]{:T(128)} %get-tuple-element.278, f32[1024]{0:T(1024)S(1)} %bitcast.123, f32[1024]{0:T(1024)S(1)} %bitcast.127, f32[1024]{0:T(1024)S(1)} %bitcast.119, f32[1024]{0:T(1024)S(1)} %bitcast.131, f32[]{:T(128)} %get-tuple-element.275, f32[]{:T(128)} %get-tuple-element.274), kind=kLoop, calls=%fused_computation.7.clone.1.clone | loop fusion | flops 15728639 | bytes 16400 | tf_op jit(solution)/shard_map/while/body/eval_jaxpr/reduce_sum | solution.py:103
  182.0 4.4 %cholesky.73 = f32[48,48]{1,0:T(8,128)S(1)} custom-call(f32[48,48]{1,0:T(8,128)S(1)} %fusion.68), custom_call_target="Cholesky" | custom-call | tf_op jit(solution)/shard_map/while/body/eval_jaxpr/jit(cholesky)/cholesky | solution.py:61
  187.7 3.7 %custom-call.20 = f32[1,48,48]{1,2,0:T(8,128)S(1)} custom-call(f32[1,48,48]{2,1,0:T(8,128)S(1)} %fusion.69), custom_call_target="InvertDiagBlocksLowerTriangular" | custom-call | tf_op jit(solution)/shard_map/while/body/eval_jaxpr/jit(_cho_solve)/triangular_solve | solution.py:62
  195.2 7.4 %multiply_reduce_fusion.7 = f32[]{:T(128)} fusion(f32[48,1024]{1,0:T(8,128)S(1)} %get-tuple-element.222, f32[48,1024]{1,0:T(8,128)S(1)} %get-tuple-element.226, f32[]{:T(128)} %get-tuple-element.278, f32[1024]{0:T(1024)S(1)} %bitcast.126, f32[1024]{0:T(1024)S(1)} %bitcast.130, f32[1024]{0:T(1024)S(1)} %bitcast.122, f32[1024]{0:T(1024)S(1)} %bitcast.134, ...), kind=kOutput, calls=%fused_computation.6.clone.1.clone | convolution fusion | flops 622854144 | bytes 409616 | tf_op jit(solution)/shard_map/while/body/eval_jaxpr/dot_general | solution.py:63
  204.0 11.7 %psum.60 = s32[]{:T(128)} all-reduce(s32[]{:T(128)} %select_reduce_fusion.2), channel_id=1, replica_groups=mesh['prow'=8,'pcol_0'=4,'pcol_1'=4,'pcol_2'=2] {'prow'}, use_global_device_ids=true, to_apply=%region_13.14 | all-reduce | flops 1 | bytes 8 | tf_op jit(solution)/shard_map/psum | solution.py:28
  215.6 11.8 %psum.56 = f32[]{:T(128)} all-reduce(f32[]{:T(128)} %fusion.22), channel_id=1, replica_groups=mesh['prow'=8,'pcol_0'=4,'pcol_1'=4,'pcol_2'=2] {'prow'}, use_global_device_ids=true, to_apply=%region_8.9 | all-reduce | flops 1 | bytes 8 | tf_op jit(solution)/shard_map/psum | solution.py:28
  227.4 6.9 %psum.61 = s32[]{:T(128)} all-reduce(s32[]{:T(128)} %psum.60), channel_id=1, replica_groups=mesh['prow'=8,'pcol_0'=4,'pcol_1'=4,'pcol_2'=2] {'pcol_0'}, use_global_device_ids=true, to_apply=%region_14.15 | all-reduce | flops 1 | bytes 8 | tf_op jit(solution)/shard_map/psum | solution.py:28
  234.3 8.1 %psum.57 = f32[]{:T(128)} all-reduce(f32[]{:T(128)} %psum.56), channel_id=1, replica_groups=mesh['prow'=8,'pcol_0'=4,'pcol_1'=4,'pcol_2'=2] {'pcol_0'}, use_global_device_ids=true, to_apply=%region_9.10 | all-reduce | flops 1 | bytes 8 | tf_op jit(solution)/shard_map/psum | solution.py:28
  242.4 6.2 %psum.62 = s32[]{:T(128)} all-reduce(s32[]{:T(128)} %psum.61), channel_id=1, replica_groups=mesh['prow'=8,'pcol_0'=4,'pcol_1'=4,'pcol_2'=2] {'pcol_1'}, use_global_device_ids=true, to_apply=%region_15.16 | all-reduce | flops 1 | bytes 8 | tf_op jit(solution)/shard_map/psum | solution.py:28
  248.6 7.7 %psum.58 = f32[]{:T(128)} all-reduce(f32[]{:T(128)} %psum.57), channel_id=1, replica_groups=mesh['prow'=8,'pcol_0'=4,'pcol_1'=4,'pcol_2'=2] {'pcol_1'}, use_global_device_ids=true, to_apply=%region_10.11 | all-reduce | flops 1 | bytes 8 | tf_op jit(solution)/shard_map/psum | solution.py:28
  256.3 16.5 %psum.63 = s32[1]{0:T(128)} all-reduce(s32[1]{0:T(128)} %bitcast.25), channel_id=1, replica_groups=mesh['prow'=8,'pcol_0'=4,'pcol_1'=4,'pcol_2'=2] {'pcol_2'}, use_global_device_ids=true, to_apply=%region_16.17 | all-reduce | flops 1 | bytes 8 | tf_op jit(solution)/shard_map/psum | solution.py:28
  (91 shorter events, 76.2 us)
Async XLA Ops:
  7.2 60.0 %copy-start = (s32[4,1,1,1]{0,3,2,1:T(1,128)S(1)}, s32[4,1,1,1]{0,3,2,1:T(1,128)}, u32[]{:S(2)}) copy-start(s32[4,1,1,1]{0,3,2,1:T(1,128)} %param.13) | copy-start | bytes 52
  7.2 57.4 %all-gather.2.cloned.1.call-start = ((), (), s32[]{:S(2)}) async-start(), calls=%async_computation.1 | async-start | bytes 3244032 | tf_op jit(solution)/shard_map/all_gather | solution.py:94
  9.4 17.5 %all-to-all-start = ((f32[32,1,1,2,1024]{4,3,2,1,0:T(2,128)}), f32[32,1,1,2,1024]{4,3,2,1,0:T(2,128)S(1)}, u32[]{:S(2)}, u32[]{:S(2)}) async-start(f32[32,1,1,2,1024]{4,3,2,1,0:T(2,128)} %broadcast_in_dim.93), calls=%async_computation | async-start | bytes 524288 | tf_op jit(solution)/shard_map/all_to_all | solution.py:19
Sparse Core Ops, SparseCore 0:
  10.5 53.9 all-gather.1
where the time goes:
time: 286 us; the launch traced here: 285 us
  blocking collectives  71.9 us (25%)
  other arithmetic  64.6 us (23%)
  matrix products  61.3 us (21%)
  waiting for transfers between devices  42.7 us (15%)
  between operations  16.2 us (6%)
  local copies, waits for them, and re-layouts  14.2 us (5%)
  starting transfers between devices  8.61 us (3%)
  loops' own time  5.85 us (2%)
    psum x8, blocking collectives, one_axis_at_a_time(): x = lax.psum(x, axis)  71.9 us
    all_gather x1, waiting for transfers between devices, per_device(): bank_whole = lax.all_gather(sketch_bank, PCOL, axis=0, tiled=True)  36.6 us
    dot_general x4, matrix products, compress(): lax.dot_general(sketched, coeffs, (((0,), (0,)), ((), ())), precision=lax...  29.4 us
    another operation x12, other arithmetic, compress(): factor = jnp.linalg.cholesky(gram)  20.2 us
    another operation x8, other arithmetic, compress(): coeffs = jax.scipy.linalg.cho_solve((factor, True), product)  17.3 us
    reduce_sum x4, other arithmetic, one_tile(): norm_sq = jnp.sum(tile_block * tile_block)  17 us
    dot_general x4, matrix products, compress(): jnp.dot(sketched.astype(jnp.bfloat16), tile_low, preferred_element_type=j...  12.7 us
    dot_general x4, matrix products, compress(): lax.dot_general(sketch, tile_low, (((1,), (1,)), ((), ())), preferred_ele...  12.6 us
  transfers between devices with their start and end apart: 2, of which 2 were waited for; matrix products, arithmetic and copies ran while one was open for 2% of the time, Pallas kernels for 0%

commit v1 on v0

--- a/solution.py
+++ b/solution.py
@@ -25,7 +25,7 @@
 
 def one_axis_at_a_time(x, axes):
     for axis in axes:
-        x = lax.psum(x, axis)
+        x = jnp.sum(lax.all_gather(x, axis), axis=0)
     return x
 
 

time: 286 us -> 265 us (0.927)
  waiting for transfers between devices: 42.7 us -> 0.7 us
  local copies, waits for them, and re-layouts: 14.2 us -> 30.3 us
  other arithmetic: 64.6 us -> 69.5 us
    psum x8 -> x0, blocking collectives: 71.9 us -> none  [one_axis_at_a_time(): x = lax.psum(x, axis)]
    unnamed x0 -> x8, blocking collectives: none -> 69.3 us
    all_gather x1, waiting for transfers between devices: 36.6 us -> 0.02 us  [per_device(): bank_whole = lax.all_gather(sketch_bank, PCOL, axis=0, tiled=True)]
    unnamed x2 -> x20, local copies, waits for them, and re-layouts: 0.01 us -> 16.1 us
    all_to_all x1, waiting for transfers between devices: 5.43 us -> 0.01 us  [sent_to_all(): return lax.all_to_all(copies, axis, split_axis=0, concat_axis=0, tiled=True)]
    reduce_sum x0 -> x8, other arithmetic: none -> 5 us  [one_axis_at_a_time(): x = jnp.sum(lax.all_gather(x, axis), axis=0)]
  transfers between devices with their start and end apart: 2 -> 2, of which waited for: 2 -> 0; matrix products, arithmetic and copies ran while one was open for 2% -> 7% of each run, Pallas kernels for 0% -> 0%
where the time goes in v1:
time: 265 us; the launch traced here: 264 us
  other arithmetic  69.5 us (26%)
  blocking collectives  69.3 us (26%)
  matrix products  61.3 us (23%)
  local copies, waits for them, and re-layouts  30.3 us (11%)
  between operations  16.2 us (6%)
  starting transfers between devices  10.7 us (4%)
  loops' own time  6.04 us (2%)
    unnamed x8, blocking collectives  69.3 us
    dot_general x4, matrix products, compress(): lax.dot_general(sketched, coeffs, (((0,), (0,)), ((), ())), precision=lax...  29.4 us
    another operation x12, other arithmetic, compress(): factor = jnp.linalg.cholesky(gram)  20.2 us
    another operation x8, other arithmetic, compress(): coeffs = jax.scipy.linalg.cho_solve((factor, True), product)  17.3 us
    reduce_sum x4, other arithmetic, one_tile(): norm_sq = jnp.sum(tile_block * tile_block)  17 us
    unnamed x20, local copies, waits for them, and re-layouts  16.1 us
    dot_general x4, matrix products, compress(): jnp.dot(sketched.astype(jnp.bfloat16), tile_low, preferred_element_type=j...  12.7 us
    dot_general x4, matrix products, compress(): lax.dot_general(sketch, tile_low, (((1,), (1,)), ((), ())), preferred_ele...  12.6 us
  transfers between devices with their start and end apart: 2, of which 0 were waited for; matrix products, arithmetic and copies ran while one was open for 7% of the time, Pallas kernels for 0%

profile of v1, /device:TPU:1, one launch (start us, length us, event | category | flops | bytes accessed | tf_op | source)
XLA Modules:
  0.0 264.0 jit_solution(12656178016808818181)
XLA Ops:
  11.8 14.0 %all-reduce.4 = s32[8]{0:T(128)S(1)} all-reduce(s32[8]{0:T(128)S(1)} %dynamic-update-slice.7), channel_id=1, replica_groups=mesh['prow'=8,'pcol_0'=4,'pcol_1'=4,'pcol_2'=2] {'prow'}, use_global_device_ids=true, to_apply=%add.4 | all-reduce | flops 8 | bytes 64
  30.5 10.6 %all-to-all-start = ((f32[32,1,1,2,1024]{4,3,2,1,0:T(2,128)}), f32[32,1,1,2,1024]{4,3,2,1,0:T(2,128)S(1)}, u32[]{:S(2)}, u32[]{:S(2)}) async-start(f32[32,1,1,2,1024]{4,3,2,1,0:T(2,128)} %broadcast_in_dim.93), calls=%async_computation | async-start | bytes 524288 | tf_op jit(solution)/shard_map/all_to_all | solution.py:19
  41.2 7.6 %all-reduce.5 = s32[4]{0:T(128)S(1)} all-reduce(s32[4]{0:T(128)S(1)} %dynamic-update-slice.8), channel_id=1, replica_groups=mesh['prow'=8,'pcol_0'=4,'pcol_1'=4,'pcol_2'=2] {'pcol_0'}, use_global_device_ids=true, to_apply=%add.5 | all-reduce | flops 4 | bytes 32
  52.9 7.3 %all-reduce.6 = s32[4]{0:T(128)S(1)} all-reduce(s32[4]{0:T(128)S(1)} %dynamic-update-slice.9), channel_id=1, replica_groups=mesh['prow'=8,'pcol_0'=4,'pcol_1'=4,'pcol_2'=2] {'pcol_1'}, use_global_device_ids=true, to_apply=%add.6 | all-reduce | flops 4 | bytes 32
  68.8 136.3 %while.16 = (s32[]{:T(128)}, f32[4,48,1024]{2,1,0:T(8,128)S(1)}, f32[4,48,1024]{2,1,0:T(8,128)S(1)}, f32[4]{0:T(128)S(1)}, f32[4]{0:T(128)S(1)}, /*index=5*/s32[...) while((s32[]{:T(128)}, f32[4,48,1024]{2,1,0:T(8,128)S(1)}, ...), condition=%wide.region_6.7_spmd, body=%wide.region_0.6_spmd.sunk | while | flops 954344128 | bytes 2675315 | solution.py:110
  71.0 4.2 %multiply_reduce_fusion.4 = f32[]{:T(128)} fusion(f32[]{:T(128)} %get-tuple-element.247, f32[1024]{0:T(1024)S(1)} %bitcast.115, f32[1024]{0:T(1024)S(1)} %bitcast.119, f32[1024]{0:T(1024)S(1)} %bitcast.111, f32[1024]{0:T(1024)S(1)} %bitcast.123, f32[]{:T(128)} %get-tuple-element.244, f32[]{:T(128)} %get-tuple-element.243), kind=kLoop, calls=%fused_computation.7.clone.1 | loop fusion | flops 15728639 | bytes 16400 | tf_op jit(solution)/shard_map/while/body/eval_jaxpr/reduce_sum | solution.py:103
  81.7 4.4 %cholesky.62 = f32[48,48]{1,0:T(8,128)S(1)} custom-call(f32[48,48]{1,0:T(8,128)S(1)} %fusion.55), custom_call_target="Cholesky" | custom-call | tf_op jit(solution)/shard_map/while/body/eval_jaxpr/jit(cholesky)/cholesky | solution.py:61
  87.4 3.7 %custom-call.17 = f32[1,48,48]{1,2,0:T(8,128)S(1)} custom-call(f32[1,48,48]{2,1,0:T(8,128)S(1)} %fusion.56), custom_call_target="InvertDiagBlocksLowerTriangular" | custom-call | tf_op jit(solution)/shard_map/while/body/eval_jaxpr/jit(_cho_solve)/triangular_solve | solution.py:62
  94.9 7.4 %multiply_reduce_fusion.5 = f32[]{:T(128)} fusion(f32[48,1024]{1,0:T(8,128)S(1)} %get-tuple-element.199, f32[48,1024]{1,0:T(8,128)S(1)} %get-tuple-element.203, f32[]{:T(128)} %get-tuple-element.247, f32[1024]{0:T(1024)S(1)} %bitcast.118, f32[1024]{0:T(1024)S(1)} %bitcast.122, f32[1024]{0:T(1024)S(1)} %bitcast.114, f32[1024]{0:T(1024)S(1)} %bitcast.126, ...), kind=kOutput, calls=%fused_computation.6.clone.1 | convolution fusion | flops 622854144 | bytes 409616 | tf_op jit(solution)/shard_map/while/body/eval_jaxpr/dot_general | solution.py:63
  105.0 4.2 %multiply_reduce_fusion.4 = f32[]{:T(128)} fusion(f32[]{:T(128)} %get-tuple-element.247, f32[1024]{0:T(1024)S(1)} %bitcast.115, f32[1024]{0:T(1024)S(1)} %bitcast.119, f32[1024]{0:T(1024)S(1)} %bitcast.111, f32[1024]{0:T(1024)S(1)} %bitcast.123, f32[]{:T(128)} %get-tuple-element.244, f32[]{:T(128)} %get-tuple-element.243), kind=kLoop, calls=%fused_computation.7.clone.1 | loop fusion | flops 15728639 | bytes 16400 | tf_op jit(solution)/shard_map/while/body/eval_jaxpr/reduce_sum | solution.py:103
  115.7 4.4 %cholesky.62 = f32[48,48]{1,0:T(8,128)S(1)} custom-call(f32[48,48]{1,0:T(8,128)S(1)} %fusion.55), custom_call_target="Cholesky" | custom-call | tf_op jit(solution)/shard_map/while/body/eval_jaxpr/jit(cholesky)/cholesky | solution.py:61
  121.4 3.7 %custom-call.17 = f32[1,48,48]{1,2,0:T(8,128)S(1)} custom-call(f32[1,48,48]{2,1,0:T(8,128)S(1)} %fusion.56), custom_call_target="InvertDiagBlocksLowerTriangular" | custom-call | tf_op jit(solution)/shard_map/while/body/eval_jaxpr/jit(_cho_solve)/triangular_solve | solution.py:62
  129.0 7.4 %multiply_reduce_fusion.5 = f32[]{:T(128)} fusion(f32[48,1024]{1,0:T(8,128)S(1)} %get-tuple-element.199, f32[48,1024]{1,0:T(8,128)S(1)} %get-tuple-element.203, f32[]{:T(128)} %get-tuple-element.247, f32[1024]{0:T(1024)S(1)} %bitcast.118, f32[1024]{0:T(1024)S(1)} %bitcast.122, f32[1024]{0:T(1024)S(1)} %bitcast.114, f32[1024]{0:T(1024)S(1)} %bitcast.126, ...), kind=kOutput, calls=%fused_computation.6.clone.1 | convolution fusion | flops 622854144 | bytes 409616 | tf_op jit(solution)/shard_map/while/body/eval_jaxpr/dot_general | solution.py:63
  139.0 4.2 %multiply_reduce_fusion.4 = f32[]{:T(128)} fusion(f32[]{:T(128)} %get-tuple-element.247, f32[1024]{0:T(1024)S(1)} %bitcast.115, f32[1024]{0:T(1024)S(1)} %bitcast.119, f32[1024]{0:T(1024)S(1)} %bitcast.111, f32[1024]{0:T(1024)S(1)} %bitcast.123, f32[]{:T(128)} %get-tuple-element.244, f32[]{:T(128)} %get-tuple-element.243), kind=kLoop, calls=%fused_computation.7.clone.1 | loop fusion | flops 15728639 | bytes 16400 | tf_op jit(solution)/shard_map/while/body/eval_jaxpr/reduce_sum | solution.py:103
  149.7 4.4 %cholesky.62 = f32[48,48]{1,0:T(8,128)S(1)} custom-call(f32[48,48]{1,0:T(8,128)S(1)} %fusion.55), custom_call_target="Cholesky" | custom-call | tf_op jit(solution)/shard_map/while/body/eval_jaxpr/jit(cholesky)/cholesky | solution.py:61
  163.0 7.4 %multiply_reduce_fusion.5 = f32[]{:T(128)} fusion(f32[48,1024]{1,0:T(8,128)S(1)} %get-tuple-element.199, f32[48,1024]{1,0:T(8,128)S(1)} %get-tuple-element.203, f32[]{:T(128)} %get-tuple-element.247, f32[1024]{0:T(1024)S(1)} %bitcast.118, f32[1024]{0:T(1024)S(1)} %bitcast.122, f32[1024]{0:T(1024)S(1)} %bitcast.114, f32[1024]{0:T(1024)S(1)} %bitcast.126, ...), kind=kOutput, calls=%fused_computation.6.clone.1 | convolution fusion | flops 622854144 | bytes 409616 | tf_op jit(solution)/shard_map/while/body/eval_jaxpr/dot_general | solution.py:63
  173.0 4.2 %multiply_reduce_fusion.4 = f32[]{:T(128)} fusion(f32[]{:T(128)} %get-tuple-element.247, f32[1024]{0:T(1024)S(1)} %bitcast.115, f32[1024]{0:T(1024)S(1)} %bitcast.119, f32[1024]{0:T(1024)S(1)} %bitcast.111, f32[1024]{0:T(1024)S(1)} %bitcast.123, f32[]{:T(128)} %get-tuple-element.244, f32[]{:T(128)} %get-tuple-element.243), kind=kLoop, calls=%fused_computation.7.clone.1 | loop fusion | flops 15728639 | bytes 16400 | tf_op jit(solution)/shard_map/while/body/eval_jaxpr/reduce_sum | solution.py:103
  183.8 4.4 %cholesky.62 = f32[48,48]{1,0:T(8,128)S(1)} custom-call(f32[48,48]{1,0:T(8,128)S(1)} %fusion.55), custom_call_target="Cholesky" | custom-call | tf_op jit(solution)/shard_map/while/body/eval_jaxpr/jit(cholesky)/cholesky | solution.py:61
  197.0 7.4 %multiply_reduce_fusion.5 = f32[]{:T(128)} fusion(f32[48,1024]{1,0:T(8,128)S(1)} %get-tuple-element.199, f32[48,1024]{1,0:T(8,128)S(1)} %get-tuple-element.203, f32[]{:T(128)} %get-tuple-element.247, f32[1024]{0:T(1024)S(1)} %bitcast.118, f32[1024]{0:T(1024)S(1)} %bitcast.122, f32[1024]{0:T(1024)S(1)} %bitcast.114, f32[1024]{0:T(1024)S(1)} %bitcast.126, ...), kind=kOutput, calls=%fused_computation.6.clone.1 | convolution fusion | flops 622854144 | bytes 409616 | tf_op jit(solution)/shard_map/while/body/eval_jaxpr/dot_general | solution.py:63
  207.1 5.1 %all-reduce.7 = s32[2]{0:T(128)S(1)} all-reduce(s32[2]{0:T(128)S(1)} %dynamic-update-slice.10), channel_id=1, replica_groups=mesh['prow'=8,'pcol_0'=4,'pcol_1'=4,'pcol_2'=2] {'pcol_2'}, use_global_device_ids=true, to_apply=%add.7 | all-reduce | flops 2 | bytes 16
  212.2 11.6 %all-reduce = f32[8]{0:T(128)S(1)} all-reduce(f32[8]{0:T(128)S(1)} %dynamic-update-slice.3), channel_id=1, replica_groups=mesh['prow'=8,'pcol_0'=4,'pcol_1'=4,'pcol_2'=2] {'prow'}, use_global_device_ids=true, to_apply=%add | all-reduce | flops 8 | bytes 64
  225.8 6.6 %all-reduce.1 = f32[4]{0:T(128)S(1)} all-reduce(f32[4]{0:T(128)S(1)} %dynamic-update-slice.4), channel_id=1, replica_groups=mesh['prow'=8,'pcol_0'=4,'pcol_1'=4,'pcol_2'=2] {'pcol_0'}, use_global_device_ids=true, to_apply=%add.1 | all-reduce | flops 4 | bytes 32
  234.4 6.9 %all-reduce.2 = f32[4]{0:T(128)S(1)} all-reduce(f32[4]{0:T(128)S(1)} %dynamic-update-slice.5), channel_id=1, replica_groups=mesh['prow'=8,'pcol_0'=4,'pcol_1'=4,'pcol_2'=2] {'pcol_1'}, use_global_device_ids=true, to_apply=%add.2 | all-reduce | flops 4 | bytes 32
  243.9 10.1 %all-reduce.3 = f32[2]{0:T(128)S(1)} all-reduce(f32[2]{0:T(128)S(1)} %dynamic-update-slice.6), channel_id=1, replica_groups=mesh['prow'=8,'pcol_0'=4,'pcol_1'=4,'pcol_2'=2] {'pcol_2'}, use_global_device_ids=true, to_apply=%add.3 | all-reduce | flops 2 | bytes 16
  (119 shorter events, 90.5 us)
Async XLA Ops:
  7.2 61.7 %copy-start = (s32[4,1,1,1]{0,3,2,1:T(1,128)S(1)}, s32[4,1,1,1]{0,3,2,1:T(1,128)}, u32[]{:S(2)}) copy-start(s32[4,1,1,1]{0,3,2,1:T(1,128)} %param.13) | copy-start | bytes 52
  7.2 59.0 %all-gather.2.cloned.1.call-start = ((), (), s32[]{:S(2)}) async-start(), calls=%async_computation.1 | async-start | bytes 3244032 | tf_op jit(solution)/shard_map/all_gather | solution.py:94
  30.5 34.4 %all-to-all-start = ((f32[32,1,1,2,1024]{4,3,2,1,0:T(2,128)}), f32[32,1,1,2,1024]{4,3,2,1,0:T(2,128)S(1)}, u32[]{:S(2)}, u32[]{:S(2)}) async-start(f32[32,1,1,2,1024]{4,3,2,1,0:T(2,128)} %broadcast_in_dim.93), calls=%async_computation | async-start | bytes 524288 | tf_op jit(solution)/shard_map/all_to_all | solution.py:19
Sparse Core Ops, SparseCore 0:
  10.5 54.0 all-gather.1
